TPU v7x, 32 devices: a whole 2x2x4 slice. The times are simulated.
32 devices in a mesh: real: 2 (over y), col: 8 (over z, x), row: 2 (over core).
Axes of the slice: x: 2, y: 2, z: 4, core: 2. Of those that a mesh axis runs over, the one named last changes fastest.
Arguments:
- theta: bfloat16 [512, 16384], P(('real', 'row'), 'col'), parts along dimension 0, may hold values from -6 to 6
- signs: int32 [32768], P(('real', 'col')), parts along dimension 0, may hold values from -1 to 1, as said below
- kept: int32 [1024], replicated, may hold values from 0 to 16383, as said below
Outputs:
- gram: float32 [4, 8, 16, 256], P(('real', 'row'), 'col'), parts along dimension 0
There are 2 independent parts, one for each index of `real`. A program takes and returns all parts, laid end to end along the dimension named above; an argument that names none is the same for every part. Nothing has to cross between parts.
Inputs may be any that keep to these rules, and one draw needn't show every extreme that they name: `signs`: each entry is -1 or 1. `kept`: 1024 distinct column indices.
All inputs are finite; a program needn't handle non-finite values.
Results may differ from a plain program's by a relative error of at most 0.0036.
Values may be sent and summed in bfloat16 or wider, within the bound.
No kernel may reach another device: no remote copies, remote signals or barrier semaphores. Data moves between devices by JAX's collectives and lax.ppermute only.
A program may use at most 64 MiB of HBM per device.

v0:
```python
import jax
import jax.numpy as jnp
from jax import lax
from jax.sharding import PartitionSpec as P

SIDE = 128
KEEP = 1024


def hadamard(order, dtype):
    indices = jnp.arange(order, dtype=jnp.int32)
    common = indices[:, None] & indices[None, :]
    parity = jnp.zeros((order, order), jnp.int32)
    for position in range(order.bit_length() - 1):
        parity = parity ^ common >> position & 1
    return (1 - 2 * parity).astype(dtype)


def against(left, right):
    return jnp.dot(left, right.T, preferred_element_type=jnp.float32)


def two_factor(spread):
    height = spread.shape[0]
    flat = spread.reshape(height * SIDE, SIDE)
    inner = jnp.dot(flat, hadamard(SIDE, jnp.bfloat16), preferred_element_type=jnp.float32).reshape(
        height, SIDE, SIDE
    )
    outer = jnp.einsum(
        "rak,aj->rjk", inner, hadamard(SIDE, jnp.float32), precision=lax.Precision.HIGHEST
    )
    return outer.reshape(height, SIDE * SIDE)


def per_device(theta, signs, kept):
    scaled = theta * signs.astype(jnp.bfloat16)[None, :]
    spread = lax.all_to_all(scaled, "col", split_axis=0, concat_axis=1, tiled=True)
    transformed = two_factor(spread) / SIDE
    sketch = jnp.take(transformed, kept, axis=1).astype(jnp.bfloat16)
    own_rows = sketch.shape[0]
    half_rows = lax.all_gather(sketch, "col", axis=0, tiled=True)
    gram = against(sketch, lax.all_gather(half_rows, "row", axis=0, tiled=True))
    return (gram / KEEP).reshape(1, 1, own_rows, gram.shape[1])


def solution(mesh):
    return jax.shard_map(
        per_device,
        mesh=mesh,
        in_specs=(P(("real", "row"), "col"), P(("real", "col")), P()),
        out_specs=P(("real", "row"), "col", None, None),
        check_vma=False,
    )
```

profile of v0, /device:TPU:0, one launch (start us, length us, event | category | flops | bytes accessed | tf_op | source)
XLA Modules:
  0.0 69.4 jit_solution(3105334876577274971)
XLA Ops:
  0.0 0.7 %convert_element_type.13 = bf16[2048]{0:T(1024)(128)(2,1)S(1)} convert(s32[2048]{0:T(1024)} %param.4) | non-fusion elementwise | flops 2048 | bytes 12288 | tf_op jit(solution)/shard_map/convert_element_type | solution.py:36
  0.7 1.9 %broadcast_multiply_fusion = bf16[128,2048]{1,0:T(8,128)(2,1)} fusion(bf16[128,2048]{1,0:T(8,128)(2,1)} %param.3, bf16[2048]{0:T(1024)(128)(2,1)S(1)} %convert_element_type.13), kind=kLoop, calls=%fused_computation.6 | loop fusion | flops 262144 | bytes 1052672 | tf_op jit(solution)/shard_map/mul | solution.py:36
  2.6 7.3 %all-to-all-start = ((bf16[8,16,2048]{2,1,0:T(8,128)(2,1)}), bf16[8,16,2048]{2,1,0:T(8,128)(2,1)S(1)}, u32[]{:S(2)}, u32[]{:S(2)}) async-start(bf16[8,16,2048]{2,1,0:T(8,128)(2,1)} %bitcast.1), calls=%async_computation | async-start | bytes 1048576 | tf_op jit(solution)/shard_map/all_to_all | solution.py:37
  9.8 0.7 compare_and_fusion
  10.5 0.7 fusion.7
  11.2 13.1 %all-to-all-done = bf16[8,16,2048]{2,1,0:T(8,128)(2,1)S(1)} async-done(((bf16[8,16,2048]{2,1,0:T(8,128)(2,1)}), bf16[8,16,2048]{2,1,0:T(8,128)(2,1)S(1)}, u32[]{:S(2)}, u32[]{:S(2)}) %all-to-all-start) | async-done | bytes 524320 | tf_op jit(solution)/shard_map/all_to_all | solution.py:37
  24.3 0.3 copy.7
  24.6 0.2 dot_general.11
  24.9 0.3 fusion.4
  25.2 1.1 %fusion = bf16[16,128,128]{2,1,0:T(8,128)(2,1)S(1)} fusion(f32[16,128,128]{2,1,0:T(8,128)S(1)} %fusion.4), kind=kOutput, calls=%fused_computation.2 | convolution fusion | flops 403570688 | bytes 1572864 | tf_op jit(solution)/shard_map/rak,aj->rjk/dot_general | solution.py:29
  26.3 3.2 %copy.13 = bf16[16,128,128]{0,2,1:T(8,128)(2,1)} copy(bf16[16,128,128]{2,1,0:T(8,128)(2,1)S(1)} %fusion) | data formatting | bytes 1048576 | tf_op jit(solution)/shard_map/div | solution.py:38
  29.5 5.6 %gather_fusion = bf16[1024,16]{1,0:T(8,128)(2,1)S(1)} fusion(bf16[16,16384]{0,1:T(8,128)(2,1)} %bitcast.18, s32[1024]{0:T(1024)S(1)} %fusion.7), kind=kCustom, calls=%fused_computation | custom fusion | bytes 69632 | tf_op jit(solution)/shard_map/jit(_take)/gather | solution.py:39
  35.1 0.2 fusion.22
  35.3 0.1 copy.10
  35.4 30.7 %all_gather.6 = bf16[128,1024]{1,0:T(8,128)(2,1)S(1)} all-gather(bf16[16,1024]{1,0:T(8,128)(2,1)S(1)} %copy.10), channel_id=1, replica_groups=mesh['real'=2,'col'=8,'row'=2] {'col'}, dimensions={0}, use_global_device_ids=true | all-gather | bytes 294912 | tf_op jit(solution)/shard_map/all_gather | solution.py:41
  66.1 2.2 %all_gather.7 = bf16[256,1024]{1,0:T(8,128)(2,1)S(1)} all-gather(bf16[128,1024]{1,0:T(8,128)(2,1)S(1)} %all_gather.6), channel_id=1, replica_groups=mesh['real'=2,'col'=8,'row'=2] {'row'}, dimensions={0}, use_global_device_ids=true | all-gather | bytes 786432 | tf_op jit(solution)/shard_map/all_gather | solution.py:42
  68.3 1.1 %fusion.1 = f32[1,1,16,256]{3,2,1,0:T(8,128)} fusion(bf16[256,1024]{1,0:T(8,128)(2,1)S(1)} %all_gather.7, bf16[1024,16]{1,0:T(8,128)(2,1)S(1)} %gather_fusion, pred[1024]{0:T(1024)(128)(4,1)S(1)} %compare_and_fusion), kind=kOutput, calls=%fused_computation.4 | convolution fusion | flops 8409088 | bytes 574464 | tf_op jit(solution)/shard_map/dot_general | solution.py:20
Async XLA Ops:
  2.6 21.8 %all-to-all-start = ((bf16[8,16,2048]{2,1,0:T(8,128)(2,1)}), bf16[8,16,2048]{2,1,0:T(8,128)(2,1)S(1)}, u32[]{:S(2)}, u32[]{:S(2)}) async-start(bf16[8,16,2048]{2,1,0:T(8,128)(2,1)} %bitcast.1), calls=%async_computation | async-start | bytes 1048576 | tf_op jit(solution)/shard_map/all_to_all | solution.py:37
where the time goes:
time: 69.8 us; the launch traced here: 69.4 us
  blocking collectives  32.9 us (47%)
  waiting for transfers between devices  13.1 us (19%)
  local copies, waits for them, and re-layouts  9.42 us (13%)
  starting transfers between devices  7.28 us (10%)
  other arithmetic  4.14 us (6%)
  matrix products  2.5 us (4%)
    all_gather x1, blocking collectives, per_device(): half_rows = lax.all_gather(sketch, 'col', axis=0, tiled=True)  30.7 us
    all_to_all x1, waiting for transfers between devices, per_device(): lax.all_to_all(scaled, 'col', split_axis=0, concat_axis=1, tiled=True)  13.1 us
    all_to_all x1, starting transfers between devices, per_device(): lax.all_to_all(scaled, 'col', split_axis=0, concat_axis=1, tiled=True)  7.28 us
    gather x1, local copies, waits for them, and re-layouts, per_device(): sketch = jnp.take(transformed, kept, axis=1).astype(jnp.bfloat16)  5.6 us
    div x1, local copies, waits for them, and re-layouts, per_device(): transformed = two_factor(spread) / SIDE  3.17 us
    all_gather x1, blocking collectives, per_device(): gram = against(sketch, lax.all_gather(half_rows, 'row', axis=0, tiled=True))  2.17 us
    mul x1, other arithmetic, per_device(): scaled = theta * signs.astype(jnp.bfloat16)[None, :]  1.86 us
  transfers between devices with their start and end apart: 1, of which 1 were waited for; matrix products, arithmetic and copies ran while one was open for 2% of the time, Pallas kernels for 0%

commit v1 on v0

--- a/solution.py
+++ b/solution.py
@@ -34,7 +34,10 @@
 
 def per_device(theta, signs, kept):
     scaled = theta * signs.astype(jnp.bfloat16)[None, :]
-    spread = lax.all_to_all(scaled, "col", split_axis=0, concat_axis=1, tiled=True)
+    spread = jnp.concatenate(
+        lax.all_to_all(jnp.stack(jnp.split(scaled, lax.axis_size("col"), axis=0)), "col", 0, 0),
+        axis=1,
+    )
     transformed = two_factor(spread) / SIDE
     sketch = jnp.take(transformed, kept, axis=1).astype(jnp.bfloat16)
     own_rows = sketch.shape[0]

time: 69.8 us -> 74 us (1.060)
  local copies, waits for them, and re-layouts: 9.42 us -> 14.4 us
  other arithmetic: 4.14 us -> 3.37 us
    unnamed x0 -> x7, local copies, waits for them, and re-layouts: none -> 4.37 us
    mul x1, other arithmetic: 1.86 us -> 1.08 us  [per_device(): scaled = theta * signs.astype(jnp.bfloat16)[None, :]]
where the time goes in v1:
time: 74 us; the launch traced here: 73.6 us
  blocking collectives  32.9 us (44%)
  local copies, waits for them, and re-layouts  14.4 us (19%)
  waiting for transfers between devices  13.1 us (18%)
  starting transfers between devices  7.28 us (10%)
  other arithmetic  3.37 us (5%)
  matrix products  2.52 us (3%)
    all_gather x1, blocking collectives, per_device(): half_rows = lax.all_gather(sketch, 'col', axis=0, tiled=True)  30.7 us
    all_to_all x1, waiting for transfers between devices, per_device(): lax.all_to_all(jnp.stack(jnp.split(scaled, lax.axis_size('col'), axis=0))...  13.1 us
    all_to_all x1, starting transfers between devices, per_device(): lax.all_to_all(jnp.stack(jnp.split(scaled, lax.axis_size('col'), axis=0))...  7.28 us
    gather x1, local copies, waits for them, and re-layouts, per_device(): sketch = jnp.take(transformed, kept, axis=1).astype(jnp.bfloat16)  5.6 us
    unnamed x7, local copies, waits for them, and re-layouts  4.37 us
    div x1, local copies, waits for them, and re-layouts, per_device(): transformed = two_factor(spread) / SIDE  3.17 us
    all_gather x1, blocking collectives, per_device(): gram = against(sketch, lax.all_gather(half_rows, 'row', axis=0, tiled=True))  2.17 us
  transfers between devices with their start and end apart: 1, of which 1 were waited for; matrix products, arithmetic and copies ran while one was open for 2% of the time, Pallas kernels for 0%

profile of v1, /device:TPU:0, one launch (start us, length us, event | category | flops | bytes accessed | tf_op | source)
XLA Modules:
  0.0 73.6 jit_solution(7993746374334305770)
XLA Ops:
  0.0 0.7 convert_element_type.13
  0.7 1.1 %broadcast_multiply_fusion = bf16[128,2048]{1,0:T(8,128)(2,1)S(1)} fusion(bf16[128,2048]{1,0:T(8,128)(2,1)} %param.3, bf16[2048]{0:T(1024)(128)(2,1)S(1)} %convert_element_type.13), kind=kLoop, calls=%fused_computation.6 | loop fusion | flops 262144 | bytes 1052672 | tf_op jit(solution)/shard_map/mul | solution.py:36
  1.8 0.6 fusion.9
  2.4 0.6 fusion.8
  3.0 0.6 fusion.7
  3.6 0.6 fusion.6
  4.3 0.6 fusion.5
  4.9 0.6 fusion.4
  5.5 0.6 fusion.3
  6.2 0.6 fusion.2
  6.8 7.3 %all-to-all-start = ((bf16[8,16,2048]{2,1,0:T(8,128)(2,1)}), bf16[8,16,2048]{2,1,0:T(8,128)(2,1)S(1)}, u32[]{:S(2)}, u32[]{:S(2)}) async-start(bf16[8,16,2048]{2,1,0:T(8,128)(2,1)} %fusion.2), calls=%async_computation | async-start | bytes 1048576 | tf_op jit(solution)/shard_map/all_to_all | solution.py:38
  14.1 0.7 compare_and_fusion
  14.7 0.7 fusion.15
  15.4 13.1 %all-to-all-done = bf16[8,16,2048]{2,1,0:T(8,128)(2,1)S(1)} async-done(((bf16[8,16,2048]{2,1,0:T(8,128)(2,1)}), bf16[8,16,2048]{2,1,0:T(8,128)(2,1)S(1)}, u32[]{:S(2)}, u32[]{:S(2)}) %all-to-all-start) | async-done | bytes 524320 | tf_op jit(solution)/shard_map/all_to_all | solution.py:38
  28.5 0.3 copy.7
  28.8 0.2 dot_general.11
  29.1 0.3 fusion.12
  29.4 1.1 %fusion = bf16[16,128,128]{2,1,0:T(8,128)(2,1)S(1)} fusion(f32[16,128,128]{2,1,0:T(8,128)S(1)} %fusion.12), kind=kOutput, calls=%fused_computation.2 | convolution fusion | flops 403570688 | bytes 1572864 | tf_op jit(solution)/shard_map/rak,aj->rjk/dot_general | solution.py:29
  30.5 3.2 %copy.13 = bf16[16,128,128]{0,2,1:T(8,128)(2,1)} copy(bf16[16,128,128]{2,1,0:T(8,128)(2,1)S(1)} %fusion) | data formatting | bytes 1048576 | tf_op jit(solution)/shard_map/div | solution.py:41
  33.7 5.6 %gather_fusion = bf16[1024,16]{1,0:T(8,128)(2,1)S(1)} fusion(bf16[16,16384]{0,1:T(8,128)(2,1)} %bitcast.49, s32[1024]{0:T(1024)S(1)} %fusion.15), kind=kCustom, calls=%fused_computation | custom fusion | bytes 69632 | tf_op jit(solution)/shard_map/jit(_take)/gather | solution.py:42
  39.3 0.2 fusion.30
  39.5 0.1 copy.10
  39.6 30.7 %all_gather.6 = bf16[128,1024]{1,0:T(8,128)(2,1)S(1)} all-gather(bf16[16,1024]{1,0:T(8,128)(2,1)S(1)} %copy.10), channel_id=1, replica_groups=mesh['real'=2,'col'=8,'row'=2] {'col'}, dimensions={0}, use_global_device_ids=true | all-gather | bytes 294912 | tf_op jit(solution)/shard_map/all_gather | solution.py:44
  70.3 2.2 %all_gather.7 = bf16[256,1024]{1,0:T(8,128)(2,1)S(1)} all-gather(bf16[128,1024]{1,0:T(8,128)(2,1)S(1)} %all_gather.6), channel_id=1, replica_groups=mesh['real'=2,'col'=8,'row'=2] {'row'}, dimensions={0}, use_global_device_ids=true | all-gather | bytes 786432 | tf_op jit(solution)/shard_map/all_gather | solution.py:45
  72.5 1.1 %fusion.1 = f32[1,1,16,256]{3,2,1,0:T(8,128)} fusion(bf16[256,1024]{1,0:T(8,128)(2,1)S(1)} %all_gather.7, bf16[1024,16]{1,0:T(8,128)(2,1)S(1)} %gather_fusion, pred[1024]{0:T(1024)(128)(4,1)S(1)} %compare_and_fusion), kind=kOutput, calls=%fused_computation.4 | convolution fusion | flops 8409088 | bytes 574464 | tf_op jit(solution)/shard_map/dot_general | solution.py:20
Async XLA Ops:
  6.8 21.8 %all-to-all-start = ((bf16[8,16,2048]{2,1,0:T(8,128)(2,1)}), bf16[8,16,2048]{2,1,0:T(8,128)(2,1)S(1)}, u32[]{:S(2)}, u32[]{:S(2)}) async-start(bf16[8,16,2048]{2,1,0:T(8,128)(2,1)} %fusion.2), calls=%async_computation | async-start | bytes 1048576 | tf_op jit(solution)/shard_map/all_to_all | solution.py:38
